TPU v7x, 32 devices: a whole 2x2x4 slice. The times are simulated.
32 devices in a mesh: prow: 8 (over y, x, core), pcol: 4 (over z).
Axes of the slice: x: 2, y: 2, z: 4, core: 2. Of those that a mesh axis runs over, the one named last changes fastest.
Arguments:
- rhs: bfloat16 [128, 64, 256], P('prow'), may hold values from -6 to 6
- blocks: bfloat16 [128, 16, 256, 256], P('prow', 'pcol'), may hold values from -0.0625 to 0.0625
- inverses: bfloat16 [128, 256, 256], P('prow'), may hold values from -1 to 2.1, as said below
- columns: int32 [128, 16], P('prow', 'pcol'), may hold values from 0 to 127, as said below
- counts: int32 [128, 4], P('prow', 'pcol'), may hold values from 0 to 4, as said below
Outputs:
- solved: bfloat16 [128, 64, 256], P('prow')
Inputs may be any that keep to these rules, and one draw needn't show every extreme that they name: `columns`: slot c of array row o names a block row k (level order) of an earlier level than that of o, with (k // 8) % 4 == c // 4, or 0 where no such block row exists; only the first counts[o, c // 4] slots of a group are used. `counts`: 0 where the group has no earlier block row (level 0 in particular); otherwise 1 or more. `inverses`: each tile is the inverse of a lower triangular diagonal block, itself lower triangular.
All inputs are finite; a program needn't handle non-finite values.
Results may differ from a plain program's by a relative error of at most 0.0054.
Values may be sent and summed in bfloat16 or wider, within the bound.
No kernel may reach another device: no remote copies, remote signals or barrier semaphores. Data moves between devices by JAX's collectives and lax.ppermute only.
A program may use at most 64 MiB of HBM per device.

v0:
```python
import jax
import jax.numpy as jnp
from jax import lax
from jax.sharding import PartitionSpec as P

LEVELS = 8
LR = 2


def body(rhs, blocks, inverses, columns, counts):
    side_count = rhs.shape[1]
    block_size = rhs.shape[2]
    prow_count = lax.axis_size("prow")
    pcol_count = lax.axis_size("pcol")
    per_level = LR * prow_count
    slot_count = columns.shape[1]
    active_mask = (jnp.arange(slot_count, dtype=jnp.int32)[None, :] < counts).astype(jnp.bfloat16)
    store_rows = LEVELS * prow_count
    solved_store = jnp.zeros((store_rows, side_count, block_size), jnp.bfloat16)
    solution = jnp.zeros(rhs.shape, jnp.bfloat16)

    def advance(level_no, carry):
        solved_store, solution = carry
        first_row = level_no * LR
        column_ids = lax.dynamic_slice_in_dim(columns, first_row, LR, 0)
        active = lax.dynamic_slice_in_dim(active_mask, first_row, LR, 0)
        panels = lax.dynamic_slice_in_dim(blocks, first_row, LR, 0)
        right_side = lax.dynamic_slice_in_dim(rhs, first_row, LR, 0)
        inverse_tiles = lax.dynamic_slice_in_dim(inverses, first_row, LR, 0)
        store_ids = column_ids // per_level * prow_count + column_ids % prow_count
        gathered = jnp.take(solved_store, store_ids, axis=0) * active[:, :, None, None]
        update_sum = jnp.einsum(
            "scrj,scij->sri", gathered, panels, preferred_element_type=jnp.float32
        )
        which_half = (lax.axis_index("pcol") - level_no * LR) % pcol_count
        keep_half = (which_half < LR).astype(jnp.bfloat16)
        half_index = jnp.minimum(which_half, LR - 1)
        summed = lax.psum(update_sum, "pcol")
        residual = (right_side.astype(jnp.float32) - summed).astype(jnp.bfloat16)
        solved_now = jnp.einsum(
            "srb,sab->sra", residual, inverse_tiles, preferred_element_type=jnp.float32
        ).astype(jnp.bfloat16)
        payload = lax.dynamic_index_in_dim(solved_now, half_index, 0, keepdims=True) * keep_half
        level_block = lax.all_gather(payload[None], "prow", axis=0, tiled=True)
        column_block = level_block.reshape((prow_count, side_count, block_size))
        solved_store = lax.dynamic_update_slice_in_dim(
            solved_store, column_block, level_no * prow_count, 0
        )
        solution = lax.dynamic_update_slice_in_dim(solution, solved_now, first_row, 0)
        return (solved_store, solution)

    solved_store, solution = lax.fori_loop(0, LEVELS, advance, (solved_store, solution))
    return solution


def solution(mesh):
    placed = (
        P("prow", None, None),
        P("prow", "pcol", None, None),
        P("prow", None, None),
        P("prow", "pcol"),
        P("prow", "pcol"),
    )
    return jax.shard_map(
        body, mesh=mesh, in_specs=placed, out_specs=P("prow", None, None), check_vma=False
    )
```

profile of v0, /device:TPU:0, one launch (start us, length us, event | category | flops | bytes accessed | tf_op | source)
XLA Modules:
  0.0 398.1 jit_solution(2024207592908420231)
XLA Ops:
  6.5 0.7 fusion.12
  7.3 0.8 copy.7
  8.1 0.2 broadcast_in_dim.57
  8.3 382.1 %while.18 = (s32[]{:T(128)}, bf16[64,64,256]{2,1,0:T(8,128)(2,1)S(1)}, bf16[16,64,256]{2,1,0:T(8,128)(2,1)S(1)}, bf16[16,64,256]{2,1,0:T(8,128)(2,1)}, s32[16,4]...) while((s32[]{:T(128)}, ...), condition=%wide.region_2.3_spmd, body=%wide.region_0.2_spmd.sunk | while | flops 84329728 | bytes 4233478 | solution.py:52
  8.4 0.1 reshape.35
  8.5 0.6 gather_fusion
  9.1 2.3 convolution_bitcast_fusion.2
  11.5 37.5 %all-reduce.2.cloned.1.call-done = f32[2,64,256]{2,1,0:T(8,128)} async-done(((f32[2,64,256]{2,1,0:T(8,128)}), f32[2,64,256]{2,1,0:T(8,128)}) %all-reduce.2.cloned.1.call-update) | async-done | bytes 131088 | tf_op jit(solution)/shard_map/while/body/eval_jaxpr/psum | solution.py:38
  49.0 1.3 constant_dynamic-update-slice_fusion.4
  50.2 9.2 %all-gather.2 = bf16[8,64,256]{2,1,0:T(8,128)(2,1)S(1)} all-gather(bf16[1,64,256]{2,1,0:T(8,128)(2,1)S(1)} %dynamic-slice_multiply_fusion.2), channel_id=2, replica_groups=mesh['prow'=8,'pcol'=4] {'prow'}, dimensions={0}, use_global_device_ids=true | all-gather | bytes 294912 | tf_op jit(solution)/shard_map/while/body/eval_jaxpr/all_gather | solution.py:44
  59.6 0.1 reshape.35
  59.7 0.6 gather_fusion
  60.3 2.3 convolution_bitcast_fusion.2
  62.7 33.6 %all-reduce.2.cloned.1.call-done = f32[2,64,256]{2,1,0:T(8,128)} async-done(((f32[2,64,256]{2,1,0:T(8,128)}), f32[2,64,256]{2,1,0:T(8,128)}) %all-reduce.2.cloned.1.call-update) | async-done | bytes 131088 | tf_op jit(solution)/shard_map/while/body/eval_jaxpr/psum | solution.py:38
  96.2 1.3 constant_dynamic-update-slice_fusion.4
  97.5 9.2 %all-gather.2 = bf16[8,64,256]{2,1,0:T(8,128)(2,1)S(1)} all-gather(bf16[1,64,256]{2,1,0:T(8,128)(2,1)S(1)} %dynamic-slice_multiply_fusion.2), channel_id=2, replica_groups=mesh['prow'=8,'pcol'=4] {'prow'}, dimensions={0}, use_global_device_ids=true | all-gather | bytes 294912 | tf_op jit(solution)/shard_map/while/body/eval_jaxpr/all_gather | solution.py:44
  106.9 0.1 reshape.35
  107.0 0.6 gather_fusion
  107.6 2.3 convolution_bitcast_fusion.2
  110.0 33.5 %all-reduce.2.cloned.1.call-done = f32[2,64,256]{2,1,0:T(8,128)} async-done(((f32[2,64,256]{2,1,0:T(8,128)}), f32[2,64,256]{2,1,0:T(8,128)}) %all-reduce.2.cloned.1.call-update) | async-done | bytes 131088 | tf_op jit(solution)/shard_map/while/body/eval_jaxpr/psum | solution.py:38
  143.5 1.3 constant_dynamic-update-slice_fusion.4
  144.8 9.2 %all-gather.2 = bf16[8,64,256]{2,1,0:T(8,128)(2,1)S(1)} all-gather(bf16[1,64,256]{2,1,0:T(8,128)(2,1)S(1)} %dynamic-slice_multiply_fusion.2), channel_id=2, replica_groups=mesh['prow'=8,'pcol'=4] {'prow'}, dimensions={0}, use_global_device_ids=true | all-gather | bytes 294912 | tf_op jit(solution)/shard_map/while/body/eval_jaxpr/all_gather | solution.py:44
  154.3 0.6 gather_fusion
  154.8 2.3 convolution_bitcast_fusion.2
  157.2 33.5 %all-reduce.2.cloned.1.call-done = f32[2,64,256]{2,1,0:T(8,128)} async-done(((f32[2,64,256]{2,1,0:T(8,128)}), f32[2,64,256]{2,1,0:T(8,128)}) %all-reduce.2.cloned.1.call-update) | async-done | bytes 131088 | tf_op jit(solution)/shard_map/while/body/eval_jaxpr/psum | solution.py:38
  190.8 1.3 constant_dynamic-update-slice_fusion.4
  192.1 9.2 %all-gather.2 = bf16[8,64,256]{2,1,0:T(8,128)(2,1)S(1)} all-gather(bf16[1,64,256]{2,1,0:T(8,128)(2,1)S(1)} %dynamic-slice_multiply_fusion.2), channel_id=2, replica_groups=mesh['prow'=8,'pcol'=4] {'prow'}, dimensions={0}, use_global_device_ids=true | all-gather | bytes 294912 | tf_op jit(solution)/shard_map/while/body/eval_jaxpr/all_gather | solution.py:44
  201.6 0.6 gather_fusion
  202.1 2.3 convolution_bitcast_fusion.2
  204.5 33.5 %all-reduce.2.cloned.1.call-done = f32[2,64,256]{2,1,0:T(8,128)} async-done(((f32[2,64,256]{2,1,0:T(8,128)}), f32[2,64,256]{2,1,0:T(8,128)}) %all-reduce.2.cloned.1.call-update) | async-done | bytes 131088 | tf_op jit(solution)/shard_map/while/body/eval_jaxpr/psum | solution.py:38
  238.1 1.3 constant_dynamic-update-slice_fusion.4
  239.3 9.2 %all-gather.2 = bf16[8,64,256]{2,1,0:T(8,128)(2,1)S(1)} all-gather(bf16[1,64,256]{2,1,0:T(8,128)(2,1)S(1)} %dynamic-slice_multiply_fusion.2), channel_id=2, replica_groups=mesh['prow'=8,'pcol'=4] {'prow'}, dimensions={0}, use_global_device_ids=true | all-gather | bytes 294912 | tf_op jit(solution)/shard_map/while/body/eval_jaxpr/all_gather | solution.py:44
  248.8 0.6 gather_fusion
  249.4 2.3 convolution_bitcast_fusion.2
  251.8 33.5 %all-reduce.2.cloned.1.call-done = f32[2,64,256]{2,1,0:T(8,128)} async-done(((f32[2,64,256]{2,1,0:T(8,128)}), f32[2,64,256]{2,1,0:T(8,128)}) %all-reduce.2.cloned.1.call-update) | async-done | bytes 131088 | tf_op jit(solution)/shard_map/while/body/eval_jaxpr/psum | solution.py:38
  285.3 1.3 constant_dynamic-update-slice_fusion.4
  286.6 9.2 %all-gather.2 = bf16[8,64,256]{2,1,0:T(8,128)(2,1)S(1)} all-gather(bf16[1,64,256]{2,1,0:T(8,128)(2,1)S(1)} %dynamic-slice_multiply_fusion.2), channel_id=2, replica_groups=mesh['prow'=8,'pcol'=4] {'prow'}, dimensions={0}, use_global_device_ids=true | all-gather | bytes 294912 | tf_op jit(solution)/shard_map/while/body/eval_jaxpr/all_gather | solution.py:44
  296.1 0.6 gather_fusion
  296.7 2.3 convolution_bitcast_fusion.2
  299.1 33.5 %all-reduce.2.cloned.1.call-done = f32[2,64,256]{2,1,0:T(8,128)} async-done(((f32[2,64,256]{2,1,0:T(8,128)}), f32[2,64,256]{2,1,0:T(8,128)}) %all-reduce.2.cloned.1.call-update) | async-done | bytes 131088 | tf_op jit(solution)/shard_map/while/body/eval_jaxpr/psum | solution.py:38
  332.6 1.3 constant_dynamic-update-slice_fusion.4
  333.9 9.2 %all-gather.2 = bf16[8,64,256]{2,1,0:T(8,128)(2,1)S(1)} all-gather(bf16[1,64,256]{2,1,0:T(8,128)(2,1)S(1)} %dynamic-slice_multiply_fusion.2), channel_id=2, replica_groups=mesh['prow'=8,'pcol'=4] {'prow'}, dimensions={0}, use_global_device_ids=true | all-gather | bytes 294912 | tf_op jit(solution)/shard_map/while/body/eval_jaxpr/all_gather | solution.py:44
  343.4 0.6 gather_fusion
  343.9 2.3 convolution_bitcast_fusion.2
  346.4 33.5 %all-reduce.2.cloned.1.call-done = f32[2,64,256]{2,1,0:T(8,128)} async-done(((f32[2,64,256]{2,1,0:T(8,128)}), f32[2,64,256]{2,1,0:T(8,128)}) %all-reduce.2.cloned.1.call-update) | async-done | bytes 131088 | tf_op jit(solution)/shard_map/while/body/eval_jaxpr/psum | solution.py:38
  379.9 1.3 constant_dynamic-update-slice_fusion.4
  381.2 9.2 %all-gather.2 = bf16[8,64,256]{2,1,0:T(8,128)(2,1)S(1)} all-gather(bf16[1,64,256]{2,1,0:T(8,128)(2,1)S(1)} %dynamic-slice_multiply_fusion.2), channel_id=2, replica_groups=mesh['prow'=8,'pcol'=4] {'prow'}, dimensions={0}, use_global_device_ids=true | all-gather | bytes 294912 | tf_op jit(solution)/shard_map/while/body/eval_jaxpr/all_gather | solution.py:44
  390.5 0.8 copy-done
  (63 shorter events, 1.6 us)
Async XLA Ops:
  8.3 40.6 %all-reduce.2.cloned.1.call-start = ((), (), s32[]{:S(2)}) async-start(), calls=%async_computation | async-start | bytes 262144 | tf_op jit(solution)/shard_map/while/body/eval_jaxpr/psum | solution.py:38
  59.5 36.7 %all-reduce.2.cloned.1.call-start = ((), (), s32[]{:S(2)}) async-start(), calls=%async_computation | async-start | bytes 262144 | tf_op jit(solution)/shard_map/while/body/eval_jaxpr/psum | solution.py:38
  106.8 36.7 %all-reduce.2.cloned.1.call-start = ((), (), s32[]{:S(2)}) async-start(), calls=%async_computation | async-start | bytes 262144 | tf_op jit(solution)/shard_map/while/body/eval_jaxpr/psum | solution.py:38
  154.1 36.7 %all-reduce.2.cloned.1.call-start = ((), (), s32[]{:S(2)}) async-start(), calls=%async_computation | async-start | bytes 262144 | tf_op jit(solution)/shard_map/while/body/eval_jaxpr/psum | solution.py:38
  201.4 36.7 %all-reduce.2.cloned.1.call-start = ((), (), s32[]{:S(2)}) async-start(), calls=%async_computation | async-start | bytes 262144 | tf_op jit(solution)/shard_map/while/body/eval_jaxpr/psum | solution.py:38
  248.6 36.7 %all-reduce.2.cloned.1.call-start = ((), (), s32[]{:S(2)}) async-start(), calls=%async_computation | async-start | bytes 262144 | tf_op jit(solution)/shard_map/while/body/eval_jaxpr/psum | solution.py:38
  295.9 36.7 %all-reduce.2.cloned.1.call-start = ((), (), s32[]{:S(2)}) async-start(), calls=%async_computation | async-start | bytes 262144 | tf_op jit(solution)/shard_map/while/body/eval_jaxpr/psum | solution.py:38
  343.2 36.7 %all-reduce.2.cloned.1.call-start = ((), (), s32[]{:S(2)}) async-start(), calls=%async_computation | async-start | bytes 262144 | tf_op jit(solution)/shard_map/while/body/eval_jaxpr/psum | solution.py:38
  390.4 0.8 copy-start
Sparse Core Ops, SparseCore 0:
  11.6 37.3 all-reduce.1
  62.8 33.4 all-reduce.1
  110.1 33.4 all-reduce.1
  157.3 33.4 all-reduce.1
  204.6 33.4 all-reduce.1
  251.9 33.4 all-reduce.1
  299.2 33.4 all-reduce.1
  346.4 33.4 all-reduce.1
where the time goes:
time: 399 us; the launch traced here: 398 us
  waiting for transfers between devices  272 us (68%)
  blocking collectives  74 us (19%)
  matrix products  28.7 us (7%)
  between operations  13.4 us (3%)
  local copies, waits for them, and re-layouts  7.25 us (2%)
    psum x8, waiting for transfers between devices, advance(): summed = lax.psum(update_sum, 'pcol')  272 us
    all_gather x8, blocking collectives, advance(): level_block = lax.all_gather(payload[None], 'prow', axis=0, tiled=True)  74 us
    dot_general x8, matrix products, advance(): jnp.einsum('scrj,scij->sri', gathered, panels, preferred_element_type=jnp...  18.7 us
    dot_general x8, matrix products, advance(): jnp.einsum('srb,sab->sra', residual, inverse_tiles, preferred_element_typ...  10 us
  transfers between devices with their start and end apart: 8, of which 8 were waited for; matrix products, arithmetic and copies ran while one was open for 0% of the time, Pallas kernels for 0%

commit v1 on v0

--- a/solution.py
+++ b/solution.py
@@ -1,10 +1,19 @@
+import functools
 import jax
 import jax.numpy as jnp
 from jax import lax
 from jax.sharding import PartitionSpec as P
+from jax.lax import all_gather
 
 LEVELS = 8
 LR = 2
+
+
+def match_block(in_array, axis_name):
+    return all_gather(in_array, axis_name=axis_name).sum(axis=0)
+
+
+trace_scenes_here = functools.partial(match_block, axis_name="pcol")
 
 
 def body(rhs, blocks, inverses, columns, counts):
@@ -35,7 +44,7 @@
         which_half = (lax.axis_index("pcol") - level_no * LR) % pcol_count
         keep_half = (which_half < LR).astype(jnp.bfloat16)
         half_index = jnp.minimum(which_half, LR - 1)
-        summed = lax.psum(update_sum, "pcol")
+        summed = trace_scenes_here(update_sum)
         residual = (right_side.astype(jnp.float32) - summed).astype(jnp.bfloat16)
         solved_now = jnp.einsum(
             "srb,sab->sra", residual, inverse_tiles, preferred_element_type=jnp.float32

time: 399 us -> 238 us (0.60)
  waiting for transfers between devices: 272 us -> 0 us
  blocking collectives: 74 us -> 205 us
  between operations: 13.4 us -> 0.03 us
  matrix products: 28.7 us -> 23 us
    psum x8 -> x0, waiting for transfers between devices: 272 us -> none  [advance(): summed = lax.psum(update_sum, 'pcol')]
    all_gather x0 -> x8, blocking collectives: none -> 134 us  [match_block(): return all_gather(in_array, axis_name=axis_name).sum(axis=0)]
    dot_general x8, matrix products: 18.7 us -> 13.4 us  [advance(): jnp.einsum('scrj,scij->sri', gathered, panels, preferred_element_type=jnp...]
  transfers between devices with their start and end apart: 8 -> 0, of which waited for: 8 -> 0; matrix products, arithmetic and copies ran while one was open for 0% -> 0% of each run, Pallas kernels for 0% -> 0%
where the time goes in v1:
time: 238 us
  blocking collectives  205 us (86%)
  matrix products  23 us (10%)
  local copies, waits for them, and re-layouts  7.25 us (3%)
    all_gather x8, blocking collectives, match_block(): return all_gather(in_array, axis_name=axis_name).sum(axis=0)  134 us
    all_gather x8, blocking collectives, advance(): level_block = lax.all_gather(payload[None], 'prow', axis=0, tiled=True)  71.4 us
    dot_general x8, matrix products, advance(): jnp.einsum('scrj,scij->sri', gathered, panels, preferred_element_type=jnp...  13.4 us
    dot_general x8, matrix products, advance(): jnp.einsum('srb,sab->sra', residual, inverse_tiles, preferred_element_typ...  9.58 us

profile of v1, /device:TPU:0, one launch (start us, length us, event | category | flops | bytes accessed | tf_op | source)
XLA Modules:
  0.0 237.6 jit_solution(15262697398195278164)
XLA Ops:
  0.0 0.7 fusion.12
  0.7 0.8 copy.7
  1.5 0.2 broadcast_in_dim.57
  1.8 235.0 %while.18 = (s32[]{:T(128)}, bf16[64,64,256]{2,1,0:T(8,128)(2,1)S(1)}, bf16[16,64,256]{2,1,0:T(8,128)(2,1)S(1)}, bf16[16,64,256]{2,1,0:T(8,128)(2,1)}, s32[16,4]...) while((s32[]{:T(128)}, ...), condition=%wide.region_2.3_spmd, body=%wide.region_0.2_spmd.sunk | while | flops 84395264 | bytes 4757738 | solution.py:61
  1.9 0.1 reshape.36
  2.0 0.6 gather_fusion
  2.6 1.7 convolution_bitcast_fusion.2
  4.2 17.4 %all-gather.4 = f32[8,64,256]{2,1,0:T(8,128)S(1)} all-gather(f32[2,64,256]{2,1,0:T(8,128)S(1)} %convolution_bitcast_fusion.2), channel_id=2, replica_groups=mesh['prow'=8,'pcol'=4] {'pcol'}, dimensions={0}, use_global_device_ids=true | all-gather | bytes 655360 | tf_op jit(solution)/shard_map/while/body/eval_jaxpr/all_gather | solution.py:13
  21.6 1.2 constant_dynamic-update-slice_fusion.4
  22.9 9.3 %all-gather.5 = bf16[8,64,256]{2,1,0:T(8,128)(2,1)S(1)} all-gather(bf16[1,64,256]{2,1,0:T(8,128)(2,1)S(1)} %dynamic-slice_multiply_fusion.2), channel_id=3, replica_groups=mesh['prow'=8,'pcol'=4] {'prow'}, dimensions={0}, use_global_device_ids=true | all-gather | bytes 294912 | tf_op jit(solution)/shard_map/while/body/eval_jaxpr/all_gather | solution.py:53
  32.3 0.1 reshape.36
  32.4 0.6 gather_fusion
  33.0 1.7 convolution_bitcast_fusion.2
  34.6 16.8 %all-gather.4 = f32[8,64,256]{2,1,0:T(8,128)S(1)} all-gather(f32[2,64,256]{2,1,0:T(8,128)S(1)} %convolution_bitcast_fusion.2), channel_id=2, replica_groups=mesh['prow'=8,'pcol'=4] {'pcol'}, dimensions={0}, use_global_device_ids=true | all-gather | bytes 655360 | tf_op jit(solution)/shard_map/while/body/eval_jaxpr/all_gather | solution.py:13
  51.5 1.2 constant_dynamic-update-slice_fusion.4
  52.7 9.3 %all-gather.5 = bf16[8,64,256]{2,1,0:T(8,128)(2,1)S(1)} all-gather(bf16[1,64,256]{2,1,0:T(8,128)(2,1)S(1)} %dynamic-slice_multiply_fusion.2), channel_id=3, replica_groups=mesh['prow'=8,'pcol'=4] {'prow'}, dimensions={0}, use_global_device_ids=true | all-gather | bytes 294912 | tf_op jit(solution)/shard_map/while/body/eval_jaxpr/all_gather | solution.py:53
  62.2 0.1 reshape.36
  62.3 0.6 gather_fusion
  62.8 1.7 convolution_bitcast_fusion.2
  64.5 16.6 %all-gather.4 = f32[8,64,256]{2,1,0:T(8,128)S(1)} all-gather(f32[2,64,256]{2,1,0:T(8,128)S(1)} %convolution_bitcast_fusion.2), channel_id=2, replica_groups=mesh['prow'=8,'pcol'=4] {'pcol'}, dimensions={0}, use_global_device_ids=true | all-gather | bytes 655360 | tf_op jit(solution)/shard_map/while/body/eval_jaxpr/all_gather | solution.py:13
  81.1 1.2 constant_dynamic-update-slice_fusion.4
  82.3 8.3 %all-gather.5 = bf16[8,64,256]{2,1,0:T(8,128)(2,1)S(1)} all-gather(bf16[1,64,256]{2,1,0:T(8,128)(2,1)S(1)} %dynamic-slice_multiply_fusion.2), channel_id=3, replica_groups=mesh['prow'=8,'pcol'=4] {'prow'}, dimensions={0}, use_global_device_ids=true | all-gather | bytes 294912 | tf_op jit(solution)/shard_map/while/body/eval_jaxpr/all_gather | solution.py:53
  90.9 0.6 gather_fusion
  91.5 1.7 convolution_bitcast_fusion.2
  93.1 16.6 %all-gather.4 = f32[8,64,256]{2,1,0:T(8,128)S(1)} all-gather(f32[2,64,256]{2,1,0:T(8,128)S(1)} %convolution_bitcast_fusion.2), channel_id=2, replica_groups=mesh['prow'=8,'pcol'=4] {'pcol'}, dimensions={0}, use_global_device_ids=true | all-gather | bytes 655360 | tf_op jit(solution)/shard_map/while/body/eval_jaxpr/all_gather | solution.py:13
  109.8 1.2 constant_dynamic-update-slice_fusion.4
  111.0 9.3 %all-gather.5 = bf16[8,64,256]{2,1,0:T(8,128)(2,1)S(1)} all-gather(bf16[1,64,256]{2,1,0:T(8,128)(2,1)S(1)} %dynamic-slice_multiply_fusion.2), channel_id=3, replica_groups=mesh['prow'=8,'pcol'=4] {'prow'}, dimensions={0}, use_global_device_ids=true | all-gather | bytes 294912 | tf_op jit(solution)/shard_map/while/body/eval_jaxpr/all_gather | solution.py:53
  120.5 0.6 gather_fusion
  121.1 1.7 convolution_bitcast_fusion.2
  122.7 16.6 %all-gather.4 = f32[8,64,256]{2,1,0:T(8,128)S(1)} all-gather(f32[2,64,256]{2,1,0:T(8,128)S(1)} %convolution_bitcast_fusion.2), channel_id=2, replica_groups=mesh['prow'=8,'pcol'=4] {'pcol'}, dimensions={0}, use_global_device_ids=true | all-gather | bytes 655360 | tf_op jit(solution)/shard_map/while/body/eval_jaxpr/all_gather | solution.py:13
  139.4 1.2 constant_dynamic-update-slice_fusion.4
  140.6 8.3 %all-gather.5 = bf16[8,64,256]{2,1,0:T(8,128)(2,1)S(1)} all-gather(bf16[1,64,256]{2,1,0:T(8,128)(2,1)S(1)} %dynamic-slice_multiply_fusion.2), channel_id=3, replica_groups=mesh['prow'=8,'pcol'=4] {'prow'}, dimensions={0}, use_global_device_ids=true | all-gather | bytes 294912 | tf_op jit(solution)/shard_map/while/body/eval_jaxpr/all_gather | solution.py:53
  149.1 0.6 gather_fusion
  149.7 1.7 convolution_bitcast_fusion.2
  151.4 16.6 %all-gather.4 = f32[8,64,256]{2,1,0:T(8,128)S(1)} all-gather(f32[2,64,256]{2,1,0:T(8,128)S(1)} %convolution_bitcast_fusion.2), channel_id=2, replica_groups=mesh['prow'=8,'pcol'=4] {'pcol'}, dimensions={0}, use_global_device_ids=true | all-gather | bytes 655360 | tf_op jit(solution)/shard_map/while/body/eval_jaxpr/all_gather | solution.py:13
  168.0 1.2 constant_dynamic-update-slice_fusion.4
  169.2 9.3 %all-gather.5 = bf16[8,64,256]{2,1,0:T(8,128)(2,1)S(1)} all-gather(bf16[1,64,256]{2,1,0:T(8,128)(2,1)S(1)} %dynamic-slice_multiply_fusion.2), channel_id=3, replica_groups=mesh['prow'=8,'pcol'=4] {'prow'}, dimensions={0}, use_global_device_ids=true | all-gather | bytes 294912 | tf_op jit(solution)/shard_map/while/body/eval_jaxpr/all_gather | solution.py:53
  178.7 0.6 gather_fusion
  179.3 1.7 convolution_bitcast_fusion.2
  181.0 16.6 %all-gather.4 = f32[8,64,256]{2,1,0:T(8,128)S(1)} all-gather(f32[2,64,256]{2,1,0:T(8,128)S(1)} %convolution_bitcast_fusion.2), channel_id=2, replica_groups=mesh['prow'=8,'pcol'=4] {'pcol'}, dimensions={0}, use_global_device_ids=true | all-gather | bytes 655360 | tf_op jit(solution)/shard_map/while/body/eval_jaxpr/all_gather | solution.py:13
  197.6 1.2 constant_dynamic-update-slice_fusion.4
  198.8 8.3 %all-gather.5 = bf16[8,64,256]{2,1,0:T(8,128)(2,1)S(1)} all-gather(bf16[1,64,256]{2,1,0:T(8,128)(2,1)S(1)} %dynamic-slice_multiply_fusion.2), channel_id=3, replica_groups=mesh['prow'=8,'pcol'=4] {'prow'}, dimensions={0}, use_global_device_ids=true | all-gather | bytes 294912 | tf_op jit(solution)/shard_map/while/body/eval_jaxpr/all_gather | solution.py:53
  207.4 0.6 gather_fusion
  207.9 1.7 convolution_bitcast_fusion.2
  209.6 16.6 %all-gather.4 = f32[8,64,256]{2,1,0:T(8,128)S(1)} all-gather(f32[2,64,256]{2,1,0:T(8,128)S(1)} %convolution_bitcast_fusion.2), channel_id=2, replica_groups=mesh['prow'=8,'pcol'=4] {'pcol'}, dimensions={0}, use_global_device_ids=true | all-gather | bytes 655360 | tf_op jit(solution)/shard_map/while/body/eval_jaxpr/all_gather | solution.py:13
  226.3 1.2 constant_dynamic-update-slice_fusion.4
  227.5 9.3 %all-gather.5 = bf16[8,64,256]{2,1,0:T(8,128)(2,1)S(1)} all-gather(bf16[1,64,256]{2,1,0:T(8,128)(2,1)S(1)} %dynamic-slice_multiply_fusion.2), channel_id=3, replica_groups=mesh['prow'=8,'pcol'=4] {'prow'}, dimensions={0}, use_global_device_ids=true | all-gather | bytes 294912 | tf_op jit(solution)/shard_map/while/body/eval_jaxpr/all_gather | solution.py:53
  236.8 0.8 copy-done
  (55 shorter events, 1.4 us)
Async XLA Ops:
  236.8 0.8 copy-start
